TPU v7x, 128 devices: a whole 4x4x4 slice. The times are simulated.
128 devices in a mesh: gx: 16 (over x, z), gy: 8 (over y, core).
Axes of the slice: x: 4, y: 4, z: 4, core: 2. Of those that a mesh axis runs over, the one named last changes fastest.
Arguments:
- tokens: bfloat16 [512, 8192], P(None, 'gx'), may hold values from -16 to 16
- attn_gain: bfloat16 [8192], P('gx'), may hold values from 0.25 to 1.75
- qkv_weight: bfloat16 [8192, 10240], P('gx', 'gy'), may hold values from -0.0625 to 0.0625
- cache_keys: bfloat16 [512, 8, 512, 128], P('gx', 'gy'), may hold values from -160 to 160
- cache_values: bfloat16 [512, 8, 512, 128], P('gx', 'gy'), may hold values from -6 to 6
- lengths: int32 [512], replicated, may hold values from 1 to 512
- live_mask: int32 [512], replicated, may hold values 0 or 1
- out_weight: bfloat16 [8192, 8192], P('gy', 'gx'), may hold values from -0.0625 to 0.0625
- mlp_gain: bfloat16 [8192], P('gx'), may hold values from 0.25 to 1.75
- gate_weight: bfloat16 [8192, 28672], P('gx', 'gy'), may hold values from -0.0625 to 0.0625
- up_weight: bfloat16 [8192, 28672], P('gx', 'gy'), may hold values from -0.0625 to 0.0625
- down_weight: bfloat16 [28672, 8192], P('gy', 'gx'), may hold values from -0.03125 to 0.03125
Outputs:
- updated: bfloat16 [512, 8192], P('gy', 'gx')
All inputs are finite; a program needn't handle non-finite values.
Results may differ from a plain program's by a relative error of at most 0.0095.
Values may be sent and summed in bfloat16 or wider, within the bound.
A program may use at most 128 MiB of HBM per device.

v0:
```python
import functools

import jax
import jax.numpy as jnp
from jax import lax
from jax.sharding import Mesh
from jax.sharding import PartitionSpec as P

D = 8192
H = 64
KVH = 8
HD = 128
GX = ("gx_0", "gx_1")


ROPE_BASE = 500000.0
NORM_EPS = 1e-05
MASKED = -1e30


def side_by_side(arrays, axis, dim, along):
    columns = [a.reshape(*a.shape[:along], -1) for a in arrays]
    both = jnp.concatenate(columns, axis=along)
    filled, at, finished = (lax.psum_scatter(both, axis, scatter_dimension=dim, tiled=True), 0, [])
    for a, column in zip(arrays, columns):
        piece = filled[..., at : at + column.shape[along]]
        finished.append(piece.reshape(*piece.shape[:along], *a.shape[along:]))
        at += column.shape[along]
    return tuple(finished)


def from_everyone(value, axis):
    length = lax.axis_size(axis)
    return lax.all_to_all(
        jnp.broadcast_to(value[None], (length, *value.shape)), axis, 0, 0, tiled=True
    )


def in_order(parts, dim):
    parts = jnp.moveaxis(parts, 0, dim)
    dims = parts.shape
    return parts.reshape(*dims[:dim], dims[dim] * dims[dim + 1], *dims[dim + 2 :])


def gather_directly(value, axis, dim):
    parts = from_everyone(value, axis)
    return in_order(parts, dim)


def gathered_total(value, axis):
    parts = lax.all_gather(value, axis)
    return parts.sum(axis=0)


def over_axes(value, axes):
    return functools.reduce(lax.psum, axes, value)


def cut_along(value, dim, length):
    dims = value.shape
    parts = value.reshape(*dims[:dim], length, dims[dim] // length, *dims[dim + 1 :])
    return jnp.moveaxis(parts, dim, 0)


def sent_and_summed(value, axis, dim):
    length = lax.axis_size(axis)
    parts = lax.all_to_all(cut_along(value, dim, length), axis, 0, 0, tiled=True)
    return jnp.sum(parts, axis=0)


def rotate_pairs(vectors, positions):
    half_width = vectors.shape[-1] // 2
    index_float = jnp.arange(half_width).astype(jnp.float32)
    inv_freq = jnp.exp(index_float * (-2.0 * jnp.log(ROPE_BASE) / vectors.shape[-1]))
    angles = positions.astype(jnp.float32)[:, None] * inv_freq[None, :]
    cosine = jnp.cos(angles)[:, None, :]
    sine_part = jnp.sin(angles)[:, None, :]
    low_half = vectors[..., :half_width]
    high_half = vectors[..., half_width:]
    return jnp.concatenate(
        (low_half * cosine - high_half * sine_part, high_half * cosine + low_half * sine_part),
        axis=-1,
    )


def make_heads(projected, square_rows, positions, groups, per_kv):
    row_count = projected.shape[0]
    attn_scale = lax.rsqrt(square_rows / D + NORM_EPS)
    shaped = (projected * attn_scale[:, None]).reshape(row_count, groups, per_kv + 2, HD)
    query_rows = rotate_pairs(
        shaped[:, :, :per_kv].reshape(row_count, groups * per_kv, HD), positions
    )
    query_rows = query_rows.astype(jnp.bfloat16).reshape(row_count, groups, per_kv, HD)
    fresh_key_rows = rotate_pairs(shaped[:, :, per_kv], positions).astype(jnp.bfloat16)
    new_values = shaped[:, :, per_kv + 1].astype(jnp.bfloat16)
    return (query_rows, fresh_key_rows, new_values)


def attend(query_rows, fresh_key_rows, new_values, cache_keys, cache_values, lengths):
    score_scale = query_rows.shape[-1] ** (-0.5)
    stored_entries = (
        jnp.einsum("bgqd,bgld->bgql", query_rows, cache_keys, preferred_element_type=jnp.float32)
        * score_scale
    )
    places = jnp.arange(cache_keys.shape[2])
    valid = places[None, None, None, :] < lengths[:, None, None, None]
    stored_entries = jnp.where(valid, stored_entries, MASKED)
    self_token = (
        jnp.einsum("bgqd,bgd->bgq", query_rows, fresh_key_rows, preferred_element_type=jnp.float32)
        * score_scale
    )
    peak = jnp.maximum(jnp.max(stored_entries, axis=-1), self_token)
    attention_probs = jnp.where(valid, jnp.exp(stored_entries - peak[..., None]), 0.0).astype(
        jnp.bfloat16
    )
    weight_sum = jnp.sum(attention_probs.astype(jnp.float32), axis=-1)
    blended_values = jnp.einsum(
        "bgql,bgld->bgqd", attention_probs, cache_values, preferred_element_type=jnp.float32
    )
    own_weight = jnp.exp(self_token - peak).astype(jnp.bfloat16).astype(jnp.float32)
    totals = weight_sum + own_weight
    blended_values = (
        blended_values + own_weight[..., None] * new_values.astype(jnp.float32)[:, :, None, :]
    )
    return (blended_values / totals[..., None]).astype(jnp.bfloat16)


def per_device(
    tokens,
    attn_gain,
    qkv_weight,
    cache_keys,
    cache_values,
    lengths,
    live_mask,
    out_weight,
    mlp_gain,
    gate_weight,
    up_weight,
    down_weight,
):
    batch_size = tokens.shape[0]
    local_rows = batch_size // lax.axis_size(GX)
    groups = cache_keys.shape[1]
    per_kv = H // KVH
    row_start = lax.axis_index(GX) * local_rows
    wide_in = tokens.astype(jnp.float32)
    scaled = (wide_in * attn_gain.astype(jnp.float32)).astype(jnp.bfloat16)
    squares = jnp.sum(wide_in * wide_in, axis=1)
    partial_sum = jnp.dot(scaled, qkv_weight, preferred_element_type=jnp.float32)
    own_proj, own_squares = side_by_side((partial_sum, squares), GX, 0, 1)
    own_lengths = lax.dynamic_slice_in_dim(lengths, row_start, local_rows, 0)
    query_rows, fresh_key_rows, new_values = make_heads(
        own_proj, own_squares, own_lengths, groups, per_kv
    )
    attn = attend(query_rows, fresh_key_rows, new_values, cache_keys, cache_values, own_lengths)
    attn = attn.reshape(local_rows, groups * per_kv * HD)
    proj_part = jnp.dot(
        gather_directly(attn, GX, 0), out_weight, preferred_element_type=jnp.float32
    )
    attn_proj = gathered_total(proj_part, "gy")
    alive_col = live_mask.astype(jnp.float32)[:, None]
    residual = (wide_in + alive_col * attn_proj).astype(jnp.bfloat16)
    resid_wide = residual.astype(jnp.float32)
    mlp_in = (resid_wide * mlp_gain.astype(jnp.float32)).astype(jnp.bfloat16)
    resid_squares = jnp.sum(resid_wide * resid_wide, axis=1)
    out_rows = batch_size // lax.axis_size("gy")
    out_start = lax.axis_index("gy") * out_rows
    square_all = over_axes(resid_squares, GX)
    hidden_width = gate_weight.shape[1]
    stacked = lax.psum_scatter(
        jnp.concatenate(
            (
                jnp.dot(mlp_in, gate_weight, preferred_element_type=jnp.float32),
                jnp.dot(mlp_in, up_weight, preferred_element_type=jnp.float32),
            ),
            axis=1,
        ),
        GX,
        scatter_dimension=0,
        tiled=True,
    )
    own_all = lax.dynamic_slice_in_dim(square_all, row_start, local_rows, 0)
    mlp_scale = lax.rsqrt(own_all / D + NORM_EPS)[:, None]
    hidden_share = (
        jax.nn.silu(stacked[:, :hidden_width] * mlp_scale) * (stacked[:, hidden_width:] * mlp_scale)
    ).astype(jnp.bfloat16)
    down_full = jnp.dot(
        lax.all_gather(hidden_share, GX, axis=0, tiled=True),
        down_weight,
        preferred_element_type=jnp.float32,
    )
    down_sum = sent_and_summed(down_full, "gy", 0)
    resid_rows = lax.dynamic_slice_in_dim(resid_wide, out_start, out_rows, 0)
    alive_rows = lax.dynamic_slice_in_dim(alive_col, out_start, out_rows, 0)
    return (resid_rows + alive_rows * down_sum).astype(jnp.bfloat16)


def solution(mesh):
    finer = Mesh(mesh.devices.reshape(4, 4, mesh.shape["gy"]), ("gx_0", "gx_1", "gy"))
    return jax.shard_map(
        per_device,
        mesh=finer,
        in_specs=(
            P(None, GX),
            P(GX),
            P(GX, "gy"),
            P(GX, "gy", None, None),
            P(GX, "gy", None, None),
            P(),
            P(),
            P("gy", GX),
            P(GX),
            P(GX, "gy"),
            P(GX, "gy"),
            P("gy", GX),
        ),
        out_specs=P("gy", GX),
        check_vma=False,
    )
```

profile of v0, /device:TPU:1, one launch (start us, length us, event | category | flops | bytes accessed | tf_op | source)
XLA Modules:
  0.0 373.0 jit_solution(5612186079310738243)
XLA Ops:
  6.5 0.0 copy-start
  6.5 0.0 reduce-scatter.3.cloned.1.call-start
  6.5 0.8 convert_element_type.82
  7.3 1.2 fusion.20
  8.5 0.1 copy.13
  8.7 0.0 copy-done
  8.7 1.9 fusion.23
  10.6 1.8 pad_maximum_fusion.1
  12.4 0.0 reduce-scatter.3.cloned.1.call-update
  12.4 0.0 all-gather.6.cloned.1.call-start
  12.5 0.8 fusion.53
  13.2 0.1 iota_compare_fusion
  13.3 0.1 multiply_cosine_fusion.1
  13.5 77.0 %reduce-scatter.3.cloned.1.call-done = f32[32,1281]{1,0:T(8,128)} async-done(((f32[512,1281]{1,0:T(8,128)}), f32[32,1281]{1,0:T(8,128)}) %reduce-scatter.3.cloned.1.call-update) | async-done | bytes 163984 | tf_op jit(solution)/shard_map/reduce_scatter | solution.py:24
  90.5 0.8 fusion.41
  91.3 1.0 slice_multiply_fusion.2
  92.4 0.0 copy-start.3
  92.5 0.1 fusion.46
  92.6 0.1 maximum_bitcast_fusion
  92.7 0.1 subtract_convert_fusion
  92.8 0.2 fusion.42
  93.0 3.8 %fusion.54 = (f32[32,8]{1,0:T(8,128)S(1)}, f32[32,8,512]{2,1,0:T(8,128)S(1)}) fusion(bf16[32,1,512,128]{3,2,1,0:T(8,128)(2,1)} %param.15, bf16[32,8,64]{2,1,0:T(8,128)(2,1)S(1)} %get-tuple-element.12, bf16[32,8,64]{2,1,0:T(8,128)(2,1)S(1)} %get-tuple-element.11, pred[32,512]{1,0:T(8,128)(4,1)S(1)} %iota_compare_fusion), kind=kOutput, calls=%fused_computation.71 | convolution fusion | flops 34078464 | bytes 4801536 | tf_op jit(solution)/shard_map/bgqd,bgld->bgql/dot_general | solution.py:102
  96.9 0.3 convert_reduce_fusion
  97.1 0.0 copy-done.3
  97.2 0.0 copy-start.7
  97.2 0.7 fusion.16
  97.9 0.0 copy-start.5
  97.9 0.0 copy-start.6
  98.0 0.1 broadcast_in_dim.26
  98.1 17.5 %all_to_all.10 = bf16[16,32,1024]{2,1,0:T(8,128)(2,1)S(1)} all-to-all(bf16[16,32,1024]{2,1,0:T(8,128)(2,1)S(1)} %broadcast_in_dim.26), channel_id=1, replica_groups=mesh['gx_0'=4,'gx_1'=4,'gy'=8] {'gx_0','gx_1'}, dimensions={0} | all-to-all | bytes 2097152 | tf_op jit(solution)/shard_map/all_to_all | solution.py:34
  115.6 0.0 copy-done.7
  115.6 1.8 fusion.55
  117.4 0.0 all-gather.6.cloned.1.call-update
  117.4 0.0 reduce-scatter.5.cloned.1.call-start
  117.4 0.0 copy-done.5
  117.5 0.0 copy-done.6
  117.5 52.0 %all-gather.6.cloned.1.call-done = f32[4096,512]{1,0:T(8,128)} async-done(((f32[512,512]{1,0:T(8,128)}), f32[4096,512]{1,0:T(8,128)}) %all-gather.6.cloned.1.call-update) | async-done | bytes 8388624 | tf_op jit(solution)/shard_map/all_gather | solution.py:51
  169.5 0.0 copy-start.2
  169.5 4.5 %reduce_sum.47 = f32[512,512]{1,0:T(8,128)S(1)} reduce(f32[8,512,512]{2,1,0:T(8,128)} %bitcast.45, f32[]{:T(128)} %constant.12.clone.1), dimensions={0}, to_apply=%region_4.5 | reduce | flops 1835008 | bytes 9437188 | tf_op jit(solution)/shard_map/reduce_sum | solution.py:52
  174.0 0.0 copy-done.2
  174.0 0.3 multiply_reduce_fusion
  174.3 0.0 copy-start.4
  174.4 4.3 %fusion.28 = f32[512,3584]{1,0:T(8,128)S(1)} fusion(bf16[512,3584]{1,0:T(8,128)(2,1)} %param.22, f32[512,512]{1,0:T(8,128)S(1)} %get-tuple-element.6, f32[512]{0:T(512)S(1)} %convert_element_type.93), kind=kOutput, calls=%fused_computation.28 | convolution fusion | flops 1879572480 | bytes 12060672 | tf_op jit(solution)/shard_map/dot_general | solution.py:175
  178.6 0.0 copy-done.4
  178.6 2.1 fusion.29
  180.7 5.5 %pad_maximum_fusion = f32[512,7168]{1,0:T(8,128)} fusion(f32[512,3584]{1,0:T(8,128)S(1)} %fusion.28, f32[512,3584]{1,0:T(8,128)S(1)} %fusion.29), kind=kLoop, calls=%fused_computation | loop fusion | flops 3670016 | bytes 29360128 | tf_op jit(solution)/shard_map/concatenate | solution.py:172
  186.2 0.0 reduce-scatter.5.cloned.1.call-update
  186.2 0.0 all-gather.4.cloned.1.call-start
  186.3 8.4 %psum.14 = f32[512]{0:T(512)S(1)} all-reduce(f32[512]{0:T(512)S(1)} %get-tuple-element.5), channel_id=1, replica_groups=mesh['gx_0'=4,'gx_1'=4,'gy'=8] {'gx_0'}, use_global_device_ids=true, to_apply=%region_7.8 | all-reduce | flops 512 | bytes 4096 | tf_op jit(solution)/shard_map/psum | solution.py:56
  194.7 9.5 %psum.15 = f32[512]{0:T(512)S(1)} all-reduce(f32[512]{0:T(512)S(1)} %psum.14), channel_id=1, replica_groups=mesh['gx_0'=4,'gx_1'=4,'gy'=8] {'gx_1'}, use_global_device_ids=true, to_apply=%region_8.9 | all-reduce | flops 512 | bytes 4096 | tf_op jit(solution)/shard_map/psum | solution.py:56
  204.2 0.1 add_rsqrt_fusion
  204.3 84.3 %reduce-scatter.5.cloned.1.call-done = f32[32,7168]{1,0:T(8,128)} async-done(((f32[512,7168]{1,0:T(8,128)}), f32[32,7168]{1,0:T(8,128)}) %reduce-scatter.5.cloned.1.call-update) | async-done | bytes 917520 | tf_op jit(solution)/shard_map/reduce_scatter | solution.py:171
  288.6 2.1 fusion.27
  290.7 0.0 all-gather.4.cloned.1.call-update
  290.7 48.3 %all-gather.4.cloned.1.call-done = bf16[512,3584]{1,0:T(8,128)(2,1)} async-done(((bf16[32,3584]{1,0:T(8,128)(2,1)}), bf16[512,3584]{1,0:T(8,128)(2,1)}) %all-gather.4.cloned.1.call-update) | async-done | bytes 3670032 | tf_op jit(solution)/shard_map/all_gather | solution.py:189
  339.0 0.0 copy-start.1
  339.0 6.3 %fusion.56 = f32[512,512]{1,0:T(8,128)} fusion(bf16[512,3584]{1,0:T(8,128)(2,1)} %all-gather.4.cloned.1.call-done, bf16[3584,512]{1,0:T(8,128)(2,1)} %param.23), kind=kOutput, calls=%fused_computation.73 | convolution fusion | flops 1879048192 | bytes 8388608 | tf_op jit(solution)/shard_map/dot_general | solution.py:188
  345.3 5.4 %all-to-all-start.1 = ((f32[8,64,512]{2,1,0:T(8,128)}), f32[8,64,512]{2,1,0:T(8,128)S(1)}, u32[]{:S(2)}, u32[]{:S(2)}) async-start(f32[8,64,512]{2,1,0:T(8,128)} %bitcast.46), calls=%async_computation.3 | async-start | bytes 2097152 | tf_op jit(solution)/shard_map/all_to_all | solution.py:67
  350.7 0.1 dynamic-slice.3
  350.8 14.9 %all-to-all-done.1 = f32[8,64,512]{2,1,0:T(8,128)S(1)} async-done(((f32[8,64,512]{2,1,0:T(8,128)}), f32[8,64,512]{2,1,0:T(8,128)S(1)}, u32[]{:S(2)}, u32[]{:S(2)}) %all-to-all-start.1) | async-done | bytes 1048608 | tf_op jit(solution)/shard_map/all_to_all | solution.py:67
  365.7 0.1 reduce_sum.49
  365.8 0.7 add_convert_fusion
  366.5 0.0 copy-done.1
  (10 shorter events, 0.1 us)
Async XLA Ops:
  6.5 2.2 copy-start
  6.5 84.0 %reduce-scatter.3.cloned.1.call-start = ((), (), s32[]{:S(2)}) async-start(), calls=%async_computation.4 | async-start | bytes 3063808 | tf_op jit(solution)/shard_map/reduce_scatter | solution.py:24
  12.4 157.1 %all-gather.6.cloned.1.call-start = ((), (), s32[]{:S(2)}) async-start(), calls=%async_computation.7 | async-start | bytes 9437184 | tf_op jit(solution)/shard_map/all_gather | solution.py:51
  92.4 4.8 %copy-start.3 = (bf16[32,1,512,128]{3,2,1,0:T(8,128)(2,1)S(1)}, bf16[32,1,512,128]{3,2,1,0:T(8,128)(2,1)}, u32[]{:S(2)}) copy-start(bf16[32,1,512,128]{3,2,1,0:T(8,128)(2,1)} %param.16) | copy-start | bytes 12582916
  97.2 18.4 %copy-start.7 = (bf16[1024,512]{1,0:T(8,128)(2,1)S(1)}, bf16[1024,512]{1,0:T(8,128)(2,1)}, u32[]{:S(2)}) copy-start(bf16[1024,512]{1,0:T(8,128)(2,1)} %param.19) | copy-start | bytes 3145732
  97.9 19.5 %copy-start.5 = (s32[512]{0:T(512)S(1)}, s32[512]{0:T(512)}, u32[]{:S(2)}) copy-start(s32[512]{0:T(512)} %param.18) | copy-start | bytes 6148
  97.9 19.5 %copy-start.6 = (bf16[512]{0:T(512)(128)(2,1)S(1)}, bf16[512]{0:T(512)(128)(2,1)}, u32[]{:S(2)}) copy-start(bf16[512]{0:T(512)(128)(2,1)} %param.20) | copy-start | bytes 3076
  117.4 171.2 %reduce-scatter.5.cloned.1.call-start = ((), (), s32[]{:S(2)}) async-start(), calls=%async_computation.5 | async-start | bytes 15597568 | tf_op jit(solution)/shard_map/reduce_scatter | solution.py:171
  169.5 4.5 %copy-start.2 = (bf16[512,512]{1,0:T(8,128)(2,1)S(1)}, bf16[512,512]{1,0:T(8,128)(2,1)}, u32[]{:S(2)}) copy-start(bf16[512,512]{1,0:T(8,128)(2,1)} %param.12) | copy-start | bytes 1572868
  174.3 4.3 %copy-start.4 = (bf16[512,3584]{1,0:T(8,128)(2,1)S(1)}, bf16[512,3584]{1,0:T(8,128)(2,1)}, u32[]{:S(2)}) copy-start(bf16[512,3584]{1,0:T(8,128)(2,1)} %param.21) | copy-start | bytes 11010052
  186.2 152.8 %all-gather.4.cloned.1.call-start = ((), (), s32[]{:S(2)}) async-start(), calls=%async_computation.6 | async-start | bytes 3899392 | tf_op jit(solution)/shard_map/all_gather | solution.py:189
  339.0 27.5 %copy-start.1 = (bf16[512,1280]{1,0:T(8,128)(2,1)S(1)}, bf16[512,1280]{1,0:T(8,128)(2,1)}, u32[]{:S(2)}) copy-start(bf16[512,1280]{1,0:T(8,128)(2,1)} %param.14) | copy-start | bytes 3932164
  345.3 20.4 %all-to-all-start.1 = ((f32[8,64,512]{2,1,0:T(8,128)}), f32[8,64,512]{2,1,0:T(8,128)S(1)}, u32[]{:S(2)}, u32[]{:S(2)}) async-start(f32[8,64,512]{2,1,0:T(8,128)} %bitcast.46), calls=%async_computation.3 | async-start | bytes 2097152 | tf_op jit(solution)/shard_map/all_to_all | solution.py:67
Sparse Core Ops, SparseCore 0:
  12.5 77.9 reduce-scatter.2
  117.5 51.9 all-gather.5
  186.4 102.1 reduce-scatter.4
  290.8 48.1 all-gather.3
where the time goes:
time: 373 us
  waiting for transfers between devices  277 us (74%)
  blocking collectives  35.4 us (9%)
  matrix products  21.1 us (6%)
  other arithmetic  20.5 us (5%)
  between operations  13.4 us (4%)
  starting transfers between devices  5.55 us (1%)
    reduce_scatter x1, waiting for transfers between devices, per_device(): lax.psum_scatter(jnp.concatenate((jnp.dot(mlp_in, gate_weight, preferred_...  84.3 us
    reduce_scatter x1, waiting for transfers between devices, side_by_side(): lax.psum_scatter(both, axis, scatter_dimension=dim, tiled=True)  77 us
    all_gather x1, waiting for transfers between devices, gathered_total(): parts = lax.all_gather(value, axis)  52 us
    all_gather x1, waiting for transfers between devices, per_device(): lax.all_gather(hidden_share, GX, axis=0, tiled=True)  48.3 us
    psum x2, blocking collectives, over_axes(): return functools.reduce(lax.psum, axes, value)  17.9 us
    all_to_all x1, blocking collectives, from_everyone(): lax.all_to_all(jnp.broadcast_to(value[None], (length, *value.shape)), axi...  17.5 us
    all_to_all x1, waiting for transfers between devices, sent_and_summed(): lax.all_to_all(cut_along(value, dim, length), axis, 0, 0, tiled=True)  14.9 us
  transfers between devices with their start and end apart: 5, of which 5 were waited for; matrix products, arithmetic and copies ran while one was open for 0% of the time, Pallas kernels for 0%

commit v1 on v0

v1 whole, which is shorter than its diff:
```python
import math

import jax
import jax.numpy as jnp
from jax import lax
from jax.experimental import pallas as pl
from jax.experimental.pallas import tpu as pltpu
from jax.sharding import Mesh
from jax.sharding import PartitionSpec as P

D = 8192
HD = 128
GX = ("x", "z")
GY = ("y", "c")
MESH = pl.DeviceIdType.MESH
F32 = jnp.float32
BF16 = jnp.bfloat16

ROPE_BASE = 500000.0
NORM_EPS = 1e-05
MASKED = -1e30

MLP_CHUNKS = 7
STRAIGHT = (0, 0, 0, 0)


def send(src, dst, send_sem, recv_sem, device):
    pltpu.make_async_remote_copy(
        src_ref=src,
        dst_ref=dst,
        send_sem=send_sem,
        recv_sem=recv_sem,
        device_id=device,
        device_id_type=MESH,
    ).start()


def wait_bytes(ref, sem):
    pltpu.make_async_copy(ref, ref, sem).wait()


class Ring:
    def __init__(self, axis):
        self.me = lax.axis_index(axis)
        self.places = [lax.rem(self.me + r, 4) for r in range(4)]
        self.right, self.far, self.left = self.places[1:]
        self.devices = [{axis: place} for place in self.places]
        self.to_right, self.to_far, self.to_left = self.devices[1:]


def scatter_direct(ring, block, into, ssem, rsem):
    for r in (2, 1, 3):
        send(block(ring.places[r]), into(r - 1), ssem, rsem, ring.devices[r])


def gather_direct(ring, whole, ssem, rsem):
    for r in (2, 1, 3):
        send(whole(ring.me), whole(ring.me), ssem, rsem(r - 1), ring.devices[r])


def scatter_start(ring, block, from_far, from_near, ssem, rsem, direct=False):
    if direct:
        for half in range(2):
            send(block(ring.far, half), from_far(half), ssem, rsem(half), ring.to_far)
        for half in range(2):
            send(block(ring.right, half), from_near(0, half), ssem, rsem(2), ring.to_right)
            send(block(ring.left, half), from_near(1, half), ssem, rsem(3), ring.to_left)
        return
    send(block(ring.far, 0), from_far(0), ssem, rsem(0), ring.to_right)
    send(block(ring.far, 1), from_far(1), ssem, rsem(1), ring.to_left)
    send(block(ring.right, 1), from_near(0, 1), ssem, rsem(2), ring.to_right)
    send(block(ring.left, 0), from_near(1, 0), ssem, rsem(3), ring.to_left)


def scatter_forward(ring, block, from_far, from_near, ssem, rsem):
    for way, place, device in ((0, ring.right, ring.to_right), (1, ring.left, ring.to_left)):
        wait_bytes(from_far(way), rsem(way))
        mine = block(place, way)
        mine[...] = (mine[...].astype(F32) + from_far(way)[...].astype(F32)).astype(BF16)
        send(mine, from_near(way, way), ssem, rsem(2 + way), device)


def scatter_finish(own, near, far, rsem):
    total = own.astype(F32)
    if far is not None:
        for way in range(2):
            wait_bytes(far(way), rsem(way))
        total = total + jnp.concatenate([far(0)[...].astype(F32), far(1)[...].astype(F32)], axis=0)
    for way in range(2):
        wait_bytes(near(way), rsem(2 + way))
    return total + near(0)[...].astype(F32) + near(1)[...].astype(F32)


def gather_start(ring, whole, block, ssem, rsem, direct=False):
    if direct:
        for half in range(2):
            send(block(ring.me, half), block(ring.me, half), ssem, rsem(2 + half), ring.to_far)
    send(whole(ring.me), whole(ring.me), ssem, rsem(0), ring.to_right)
    send(whole(ring.me), whole(ring.me), ssem, rsem(1), ring.to_left)


def gather_forward(ring, whole, block, ssem, rsem):
    wait_bytes(whole(ring.left), rsem(0))
    send(block(ring.left, 0), block(ring.left, 0), ssem, rsem(2), ring.to_right)
    wait_bytes(whole(ring.right), rsem(1))
    send(block(ring.right, 1), block(ring.right, 1), ssem, rsem(3), ring.to_left)


def gather_finish(ring, whole, block, rsem, direct=False):
    if direct:
        wait_bytes(whole(ring.left), rsem(0))
        wait_bytes(whole(ring.right), rsem(1))
    wait_bytes(block(ring.far, 0), rsem(2))
    wait_bytes(block(ring.far, 1), rsem(3))


def greet(devices):
    barrier = pltpu.get_barrier_semaphore()
    for device in devices:
        pl.semaphore_signal(barrier, inc=1, device_id=device, device_id_type=MESH)
    return lambda: pl.semaphore_wait(barrier, len(devices))


def row_squares(wide):
    squares = wide * wide
    high = squares.astype(BF16)
    low = (squares - high.astype(F32)).astype(BF16)
    ones = jnp.ones((8, wide.shape[1]), BF16)
    dims = (((1,), (1,)), ((), ()))
    return lax.dot_general(ones, high, dims, preferred_element_type=F32) + lax.dot_general(
        ones, low, dims, preferred_element_type=F32
    )


def as_column(lanes, count, first):
    shape = (count, lanes.shape[1])
    lane = lax.broadcasted_iota(jnp.int32, shape, 1)
    row = lax.broadcasted_iota(jnp.int32, shape, 0)
    return jnp.sum(jnp.where(lane == row + first, lanes, 0.0), axis=1, keepdims=True)


class Squares:
    def __init__(self, rings, sq, sq_x, sq_mid, sq_z, sems):
        self.rings, self.refs, self.sems = rings, (sq, sq_x, sq_mid, sq_z), sems

    def over_x(self):
        sq, sq_x, _, _ = self.refs
        scatter_direct(
            self.rings[0], lambda d: sq.at[d], lambda i: sq_x.at[i], self.sems.at[0], self.sems.at[1]
        )

    def over_z(self):
        sq, sq_x, sq_mid, sq_z = self.refs
        wait_bytes(sq_x, self.sems.at[1])
        sq_mid[...] = sq[self.rings[0].me] + jnp.sum(sq_x[...], axis=0)
        scatter_direct(
            self.rings[1], lambda d: sq_mid, lambda i: sq_z.at[i], self.sems.at[2], self.sems.at[3]
        )

    def scale(self):
        _, _, sq_mid, sq_z = self.refs
        wait_bytes(sq_z, self.sems.at[3])
        total = sq_mid[...] + jnp.sum(sq_z[...], axis=0)
        sums = as_column(total[0:1, :], 32, 32 * self.rings[1].me)
        return lax.rsqrt(sums / D + NORM_EPS)

    def drain(self):
        wait_bytes(self.refs[1], self.sems.at[0])
        wait_bytes(self.refs[3], self.sems.at[2])


def either(k, chunks, straight, work):
    if straight == 0:
        work(False)
        return

    @pl.when(k < chunks - straight)
    def _():
        work(False)

    @pl.when(k >= chunks - straight)
    def _():
        work(True)


def run_stages(count, stages):
    def body(t, carry):
        for lag, stage in enumerate(stages):
            k = t - lag

            @pl.when((k >= 0) & (k < count))
            def _():
                stage(k)

        return carry

    lax.fori_loop(0, count + len(stages) - 1, body, 0)


def scatter_stages(rings, part, far1, near1, sum1, far2, near2, ssem, rsem):
    def block1(h, k):
        return lambda d, half: part.at[h, k, d, pl.ds(2 * half, 2)]

    def far_in1(h, k):
        return lambda way: far1.at[h, k, way]

    def near_in1(h, k):
        return lambda way, half: near1.at[h, k, way, pl.ds(2 * half, 2)]

    def block2(h, k):
        return lambda d, half: sum1.at[h, k, d, pl.ds(16 * half, 16)]

    def far_in2(h, k):
        return lambda way: far2.at[h, k, way]

    def near_in2(h, k):
        return lambda way, half: near2.at[h, k, way, pl.ds(16 * half, 16)]

    def rs(h, k, base):
        return lambda i: rsem.at[k, h, base + i]

    chunks = part.shape[1]

    def start1(k):
        def work(direct):
            for h in range(2):
                refs = (block1(h, k), far_in1(h, k), near_in1(h, k))
                scatter_start(rings[h], *refs, ssem.at[k, h, 0], rs(h, k, 0), direct)

        either(k, chunks, STRAIGHT[0], work)

    def forward1(k):
        @pl.when(k < chunks - STRAIGHT[0])
        def _():
            for h in range(2):
                refs = (block1(h, k), far_in1(h, k), near_in1(h, k))
                scatter_forward(rings[h], *refs, ssem.at[k, h, 0], rs(h, k, 0))

    def start2(k):
        def total(direct):
            for h in range(2):
                own = part[h, k, rings[h].me]
                far = far_in1(h, k) if direct else None
                got = scatter_finish(own, lambda way: near1.at[h, k, way], far, rs(h, k, 0))
                sum1[h, k] = got.astype(BF16)

        def work(direct):
            for h in range(2):
                refs = (block2(h, k), far_in2(h, k), near_in2(h, k))
                scatter_start(rings[1 - h], *refs, ssem.at[k, h, 1], rs(h, k, 4), direct)

        either(k, chunks, STRAIGHT[0], total)
        either(k, chunks, STRAIGHT[1], work)

    def forward2(k):
        @pl.when(k < chunks - STRAIGHT[1])
        def _():
            for h in range(2):
                refs = (block2(h, k), far_in2(h, k), near_in2(h, k))
                scatter_forward(rings[1 - h], *refs, ssem.at[k, h, 1], rs(h, k, 4))

    def finish2(h, k, direct):
        own = sum1[h, k, rings[1 - h].me]
        far = far_in2(h, k) if direct else None
        return scatter_finish(own, lambda way: near2.at[h, k, way], far, rs(h, k, 4))

    return start1, forward1, start2, forward2, finish2


def scatter_scratch(chunks, width):
    return [
        pltpu.VMEM((2, chunks, 4, 4, 32, width), BF16),
        pltpu.VMEM((2, chunks, 2, 2, 32, width), BF16),
        pltpu.VMEM((2, chunks, 2, 4, 32, width), BF16),
        pltpu.VMEM((2, chunks, 4, 32, width), BF16),
        pltpu.VMEM((2, chunks, 2, 16, width), BF16),
        pltpu.VMEM((2, chunks, 2, 32, width), BF16),
    ]


def gather_stages(rings, buf, ssem, rsem):
    def inner(h, k):
        ring = rings[1 - h]
        row = rings[h].me
        return (
            ring,
            lambda d: buf(h, k).at[row, d],
            lambda d, half: buf(h, k).at[row, d, pl.ds(16 * half, 16)],
        )

    def outer(h, k):
        return (
            rings[h],
            lambda d: buf(h, k).at[d],
            lambda d, half: buf(h, k).at[d, pl.ds(2 * half, 2)],
        )

    chunks = MLP_CHUNKS

    def start1(h, k, direct):
        ring, whole, block = inner(h, k)
        gather_start(ring, whole, block, ssem(h, k, 0), lambda i: rsem(h, k, i), direct)

    def forward1(k):
        @pl.when(k < chunks - STRAIGHT[2])
        def _():
            for h in range(2):
                ring, whole, block = inner(h, k)
                gather_forward(ring, whole, block, ssem(h, k, 0), lambda i: rsem(h, k, i))

    def start2(k):
        def finish(direct):
            for h in range(2):
                ring, whole, block = inner(h, k)
                gather_finish(ring, whole, block, lambda i: rsem(h, k, i), direct)

        def work(direct):
            for h in range(2):
                ring, whole, block = outer(h, k)
                gather_start(ring, whole, block, ssem(h, k, 1), lambda i: rsem(h, k, 4 + i), direct)

        either(k, chunks, STRAIGHT[2], finish)
        either(k, chunks, STRAIGHT[3], work)

    def forward2(k):
        @pl.when(k < chunks - STRAIGHT[3])
        def _():
            for h in range(2):
                ring, whole, block = outer(h, k)
                gather_forward(ring, whole, block, ssem(h, k, 1), lambda i: rsem(h, k, 4 + i))

    def finish2(k):
        def finish(direct):
            for h in range(2):
                ring, whole, block = outer(h, k)
                gather_finish(ring, whole, block, lambda i: rsem(h, k, 4 + i), direct)

        either(k, chunks, STRAIGHT[3], finish)

    def drain(h, k):
        wait_bytes(buf(h, k).at[0, pl.ds(0, 3)], ssem(h, k, 0))
        wait_bytes(buf(h, k).at[pl.ds(0, 3)], ssem(h, k, 1))

    return start1, forward1, start2, forward2, finish2, drain


def columns_sum(acc, full, mine, core_in, ring, y_in, ssem, rsem):
    core = lax.axis_index("c")
    for b in range(16):
        a, c = divmod(b, 4)
        both = acc[0, a, c] + acc[1, c, a]
        full[(b // 2) % 2, b // 4, pl.ds(32 * (b % 2), 32)] = both.astype(BF16)
    for r in (2, 1, 3, 0):
        place = ring.places[r]
        send(full.at[1 - core, place], core_in.at[place], ssem.at[0], rsem.at[r], {"c": 1 - core})
    for r in (2, 1, 3, 0):
        place = ring.places[r]
        wait_bytes(core_in.at[place], rsem.at[r])
        both = full[core, place].astype(F32) + core_in[place].astype(F32)
        if r == 0:
            total = both
        else:
            mine[place] = both.astype(BF16)
            send(mine.at[place], y_in.at[r - 1], ssem.at[1], rsem.at[4], ring.devices[r])
    wait_bytes(y_in, rsem.at[4])
    total = total + jnp.sum(y_in[...].astype(F32), axis=0)
    wait_bytes(core_in, ssem.at[0])
    wait_bytes(y_in, ssem.at[1])
    return total


def gather_plane(rings, buf, ssem, rsem):
    def block(h, r):
        return buf.at[h, rings[h].me, rings[1 - h].places[r]]

    def outward(h, r):
        for way in (2, 1, 3):
            send(block(h, r), block(h, r), ssem.at[h], rsem.at[h, 2 + way], rings[h].devices[way])

    for h in range(2):
        for way in (2, 1, 3):
            device = rings[1 - h].devices[way]
            send(block(h, 0), block(h, 0), ssem.at[h], rsem.at[h, way - 1], device)
    for h in range(2):
        outward(h, 0)
    for way in (1, 3, 2):
        for h in range(2):
            wait_bytes(block(h, 4 - way), rsem.at[h, way - 1])
            outward(h, 4 - way)

    def finish(h):
        for way in (1, 3, 2):
            wait_bytes(buf.at[h, rings[h].places[4 - way]], rsem.at[h, 2 + way])

    def drain(h):
        wait_bytes(buf.at[h, 0, pl.ds(0, 3)], ssem.at[h])
        wait_bytes(buf.at[h, pl.ds(0, 3)], ssem.at[h])

    return finish, drain


def rotation(places):
    lane = lax.broadcasted_iota(jnp.int32, (1, HD), 1)
    index = lax.rem(lane, HD // 2).astype(F32)
    inv_freq = jnp.exp(index * (-2.0 * math.log(ROPE_BASE) / HD))
    angles = places * inv_freq
    sine = jnp.sin(angles)
    return jnp.cos(angles), jnp.where(lane < HD // 2, -sine, sine)


def layer_kernel(
    tok,
    attn_gain,
    mlp_gain,
    lengths,
    live_mask,
    w_qkv,
    keys,
    values,
    w_out,
    w_gate,
    w_up,
    w_down,
    base,
    extra,
    v_tok,
    v_qkv,
    v_keys,
    v_values,
    v_out,
    v_gate,
    v_up,
    v_down,
    q_part,
    q_in1,
    q_sum1,
    q_in2,
    sq0,
    sq0_x,
    sq0_mid,
    sq0_z,
    query,
    fresh,
    attended,
    lhs,
    abuf,
    acc,
    full,
    mine,
    core_in,
    y_in,
    full2,
    mine2,
    core_in2,
    y_in2,
    resid,
    part,
    far1,
    near1,
    sum1,
    far2,
    near2,
    hid,
    sq,
    sq_x,
    sq_mid,
    sq_z,
    scales,
    wsem,
    q_ssem,
    q_rsem,
    sqs0,
    a_ssem,
    a_rsem,
    y_ssem,
    y_rsem,
    r_ssem,
    r_rsem,
    sqs,
    m_ssem,
    m_rsem,
):
    rings = (Ring("x"), Ring("z"))
    yring = Ring("y")
    core = lax.axis_index("c")
    chunks, width = part.shape[1], part.shape[5]
    cut = width // 2
    depth = lhs.shape[4]
    slot0 = 32 * (4 * rings[0].me + rings[1].me)
    row0 = 64 * (2 * yring.me + core)
    loads = [
        pltpu.make_async_copy(src, dst, wsem.at[i])
        for i, (src, dst) in enumerate(
            (
                (tok, v_tok),
                (w_qkv, v_qkv),
                (keys, v_keys),
                (values, v_values),
                (w_out, v_out),
                (w_gate, v_gate),
                (w_up, v_up),
                (w_down, v_down),
            )
        )
    ]
    loads[0].start()
    loads[1].start()
    met = greet(
        [*rings[0].devices[1:], *rings[1].devices[1:], *yring.devices[1:], {"c": 1 - core}]
    )

    def row(ref):
        return ref[...].astype(F32).reshape(1, ref.shape[0])

    def normed(a, wide, gain, squares):
        squares[a] = row_squares(wide)
        scaled = (wide * gain).astype(BF16).reshape(4, 32, depth)
        lhs[0, a] = scaled
        for b in range(4):
            lhs[1, b, a] = scaled[b]

    loads[0].wait()
    for a in range(4):
        normed(a, v_tok[128 * a : 128 * (a + 1), :].astype(F32), row(attn_gain), sq0)
    loads[1].wait()
    for load in loads[2:]:
        load.start()
    q_width = q_part.shape[4]
    for h in range(2):
        columns = slice(h * q_width, (h + 1) * q_width)
        got = jnp.dot(lhs[h].reshape(512, depth), v_qkv[:, columns], preferred_element_type=F32)
        q_part[h] = got.astype(BF16).reshape(4, 4, 32, q_width)
    squares0 = Squares(rings, sq0, sq0_x, sq0_mid, sq0_z, sqs0)
    squares = Squares(rings, sq, sq_x, sq_mid, sq_z, sqs)
    met()
    for h in range(2):
        scatter_direct(
            rings[h],
            lambda d: q_part.at[h, d],
            lambda i: q_in1.at[h, i],
            q_ssem.at[h, 0],
            q_rsem.at[h, 0],
        )
    squares0.over_x()
    places = as_column(row(lengths), 32, slot0)
    cosine, sine = rotation(places)
    squares0.over_z()
    for h in range(2):
        wait_bytes(q_in1.at[h], q_rsem.at[h, 0])
        total = q_part[h, rings[h].me].astype(F32)
        for i in range(3):
            total = total + q_in1[h, i].astype(F32)
        q_sum1[h] = total.astype(BF16)
        scatter_direct(
            rings[1 - h],
            lambda d: q_sum1.at[h, d],
            lambda i: q_in2.at[h, i],
            q_ssem.at[h, 1],
            q_rsem.at[h, 1],
        )
    scale = squares0.scale()
    for h in range(2):
        wait_bytes(q_in2.at[h], q_rsem.at[h, 1])
        total = q_sum1[h, rings[1 - h].me].astype(F32)
        for i in range(3):
            total = total + q_in2[h, i].astype(F32)
        sums = total * scale
        for i in range(5):
            column = sums[:, 128 * i : 128 * (i + 1)]
            head = 5 * h + i
            if head < 9:
                column = column * cosine + pltpu.roll(column, HD // 2, 1) * sine
            column = column.astype(BF16).astype(F32)
            if head < 8:
                query[:, head, :] = column
            else:
                fresh[:, head - 8, :] = column
    fresh[:, 2, :] = jnp.broadcast_to(places, (32, 128))

    loads[2].wait()
    loads[3].wait()

    def slots(g, carry):
        first = 8 * g
        score_scale = HD ** (-0.5)
        q = query[pl.ds(first, 8)]
        scores = []
        for i in range(8):
            scores.append(
                lax.dot_general(
                    q[i].astype(BF16),
                    v_keys[first + i],
                    (((1,), (1,)), ((), ())),
                    preferred_element_type=F32,
                )
            )
        scores = jnp.concatenate(scores, axis=0) * score_scale
        new = fresh[pl.ds(first, 8)]
        q = q.reshape(64, HD)

        def spread(i):
            return jnp.broadcast_to(new[:, i : i + 1, :], (8, 8, HD)).reshape(64, HD)

        own = jnp.sum(q * spread(0), axis=1, keepdims=True) * score_scale
        ends = spread(2)[:, 0:1]
        spot = lax.broadcasted_iota(jnp.int32, scores.shape, 1).astype(F32)
        valid = spot < ends
        scores = jnp.where(valid, scores, MASKED)
        peak = jnp.maximum(jnp.max(scores, axis=1, keepdims=True), own)
        probs = jnp.where(valid, jnp.exp(scores - peak), 0.0).astype(BF16).astype(F32)
        own_weight = jnp.exp(own - peak).astype(BF16).astype(F32)
        totals = jnp.sum(probs, axis=1, keepdims=True) + own_weight
        blends = []
        for i in range(8):
            blends.append(
                jnp.dot(
                    probs[8 * i : 8 * (i + 1)].astype(BF16),
                    v_values[first + i],
                    preferred_element_type=F32,
                )
            )
        blend = jnp.concatenate(blends, axis=0) + own_weight * spread(1)
        attended[pl.ds(first, 8)] = (blend / totals).reshape(8, 8, HD)
        return carry

    lax.fori_loop(0, 4, slots, 0)
    for head in range(8):
        h, i = divmod(head, 4)
        abuf[h, rings[h].me, rings[1 - h].me, :, 128 * i : 128 * (i + 1)] = attended[
            :, head, :
        ].astype(BF16)

    a_finish, a_drain = gather_plane(rings, abuf, a_ssem, a_rsem)
    for h in range(2):
        a_finish(h)
        if h == 0:
            loads[4].wait()
        half = abuf.shape[4]
        block = abuf[h].reshape(512, half)
        got = jnp.dot(block, v_out[h * half : (h + 1) * half, :], preferred_element_type=F32)
        acc[h] = got.reshape(4, 4, 32, acc.shape[4])
    total = columns_sum(acc, full, mine, core_in, yring, y_in, y_ssem.at[0], y_rsem.at[0])
    live = as_column(row(live_mask), 64, row0)
    kept = (v_tok[pl.ds(pl.multiple_of(row0, 64), 64), :].astype(F32) + live * total).astype(BF16)

    def r_whole(d):
        return resid.at[d, core]

    def to_core(d):
        send(r_whole(d), r_whole(d), r_ssem.at[1], r_rsem.at[3], {"c": 1 - core})

    resid[yring.me, core] = kept
    gather_direct(yring, r_whole, r_ssem.at[0], lambda i: r_rsem.at[i])
    to_core(yring.me)
    for r in (1, 3, 2):
        wait_bytes(r_whole(yring.places[4 - r]), r_rsem.at[r - 1])
        to_core(yring.places[4 - r])
    wait_bytes(resid.at[:, 1 - core], r_rsem.at[3])

    for a in range(4):
        normed(a, resid[a].astype(F32).reshape(128, depth), row(mlp_gain), sq)
    squares.over_x()
    acc[...] = jnp.zeros_like(acc)
    for load in loads[5:]:
        load.wait()

    s_start1, s_forward1, s_start2, s_forward2, s_finish2 = scatter_stages(
        rings, part, far1, near1, sum1, far2, near2, m_ssem, m_rsem
    )
    g_start1, g_forward1, g_start2, g_forward2, g_finish2, g_drain = gather_stages(
        rings,
        lambda h, k: hid.at[h, k],
        lambda h, k, i: m_ssem.at[k, h, 2 + i],
        lambda h, k, i: m_rsem.at[k, h, 8 + i],
    )

    def compute(k):
        for h in range(2):
            cols = pl.ds(pl.multiple_of((2 * k + h) * cut, 128), cut)
            block = lhs[h].reshape(512, depth)
            for i, v in enumerate((v_gate, v_up)):
                got = jnp.dot(block, v[:, cols], preferred_element_type=F32)
                part[h, k, :, :, :, i * cut : (i + 1) * cut] = got.astype(BF16).reshape(
                    4, 4, 32, cut
                )
        s_start1(k)

    def hidden(k):
        @pl.when(k == 0)
        def _():
            scales[...] = jnp.broadcast_to(squares.scale(), scales.shape)

        scale = scales[:, 0:1]

        def work(direct):
            for h in range(2):
                sums = s_finish2(h, k, direct) * scale
                gate = sums[:, :cut]
                up = sums[:, cut:]
                made = gate * (1.0 / (1.0 + jnp.exp(-gate))) * up
                hid[h, k, rings[h].me, rings[1 - h].me] = made.astype(BF16)

        def go(direct):
            for h in range(2):
                g_start1(h, k, direct)

        either(k, chunks, STRAIGHT[1], work)
        either(k, chunks, STRAIGHT[2], go)

    def down(k):
        g_finish2(k)
        for h in range(2):
            depths = pl.ds(pl.multiple_of((2 * k + h) * cut, 128), cut)
            block = hid[h, k].reshape(512, cut)
            got = jnp.dot(block, v_down[depths, :], preferred_element_type=F32)
            acc[h] += got.reshape(4, 4, 32, acc.shape[4])

    def forward1(k):
        @pl.when(k == 0)
        def _():
            squares.over_z()

        s_forward1(k)

    run_stages(
        chunks,
        (compute, forward1, s_start2, s_forward2, hidden, g_forward1, g_start2, g_forward2, down),
    )

    total = columns_sum(acc, full2, mine2, core_in2, yring, y_in2, y_ssem.at[1], y_rsem.at[1])
    base[...] = kept
    extra[...] = live * total

    squares0.drain()
    squares.drain()
    for h in range(2):
        a_drain(h)
        wait_bytes(q_in1.at[h], q_ssem.at[h, 0])
        wait_bytes(q_in2.at[h], q_ssem.at[h, 1])
    wait_bytes(resid.at[pl.ds(0, 3), 0], r_ssem.at[0])
    wait_bytes(resid.at[:, 0], r_ssem.at[1])

    def drain(k, carry):
        for h in range(2):
            wait_bytes(part.at[h, k, pl.ds(0, 3)], m_ssem.at[k, h, 0])
            wait_bytes(sum1.at[h, k, pl.ds(0, 3)], m_ssem.at[k, h, 1])
            g_drain(h, k)
        return carry

    lax.fori_loop(0, chunks, drain, 0)


def layer_rows(tok, attn_gain, mlp_gain, lengths, live_mask, w_qkv, keys, values, w_out, w_gate, w_up, w_down):
    depth = w_gate.shape[0]
    cut = w_gate.shape[1] // (2 * MLP_CHUNKS)
    half = w_out.shape[0] // 2
    across = w_out.shape[1]
    slots = keys.shape[0]
    q_width = w_qkv.shape[1] // 2
    vmem = pl.BlockSpec(memory_space=pltpu.VMEM)
    hbm = pl.BlockSpec(memory_space=pl.ANY)
    held = (tok, w_qkv, keys, values, w_out, w_gate, w_up, w_down)
    squares = [
        pltpu.VMEM((4, 8, 128), F32),
        pltpu.VMEM((3, 8, 128), F32),
        pltpu.VMEM((8, 128), F32),
        pltpu.VMEM((3, 8, 128), F32),
    ]
    sums = [
        pltpu.VMEM((2, 4, 64, across), BF16),
        pltpu.VMEM((4, 64, across), BF16),
        pltpu.VMEM((4, 64, across), BF16),
        pltpu.VMEM((3, 64, across), BF16),
    ]
    return pl.pallas_call(
        layer_kernel,
        name="layer_rows",
        out_shape=(
            jax.ShapeDtypeStruct((64, across), BF16),
            jax.ShapeDtypeStruct((64, across), F32),
        ),
        in_specs=[hbm] + [vmem] * 4 + [hbm] * 7,
        out_specs=(vmem, vmem),
        scratch_shapes=[
            *[pltpu.VMEM(a.shape, BF16) for a in held],
            pltpu.VMEM((2, 4, 4, 32, q_width), BF16),
            pltpu.VMEM((2, 3, 4, 32, q_width), BF16),
            pltpu.VMEM((2, 4, 32, q_width), BF16),
            pltpu.VMEM((2, 3, 32, q_width), BF16),
            *squares,
            pltpu.VMEM((slots, 8, HD), F32),
            pltpu.VMEM((slots, 8, HD), F32),
            pltpu.VMEM((slots, 8, HD), F32),
            pltpu.VMEM((2, 4, 4, 32, depth), BF16),
            pltpu.VMEM((2, 4, 4, 32, half), BF16),
            pltpu.VMEM((2, 4, 4, 32, across), F32),
            *sums,
            *sums,
            pltpu.VMEM((4, 2, 64, across), BF16),
            *scatter_scratch(MLP_CHUNKS, 2 * cut),
            pltpu.VMEM((2, MLP_CHUNKS, 4, 4, 32, cut), BF16),
            *squares,
            pltpu.VMEM((32, 128), F32),
            pltpu.SemaphoreType.DMA((8,)),
            pltpu.SemaphoreType.DMA((2, 2)),
            pltpu.SemaphoreType.DMA((2, 2)),
            pltpu.SemaphoreType.DMA((4,)),
            pltpu.SemaphoreType.DMA((2,)),
            pltpu.SemaphoreType.DMA((2, 6)),
            pltpu.SemaphoreType.DMA((2, 2)),
            pltpu.SemaphoreType.DMA((2, 5)),
            pltpu.SemaphoreType.DMA((2,)),
            pltpu.SemaphoreType.DMA((4,)),
            pltpu.SemaphoreType.DMA((4,)),
            pltpu.SemaphoreType.DMA((MLP_CHUNKS, 2, 4)),
            pltpu.SemaphoreType.DMA((MLP_CHUNKS, 2, 16)),
        ],
        compiler_params=pltpu.CompilerParams(
            collective_id=0, has_side_effects=True, vmem_limit_bytes=60 * 1024 * 1024
        ),
    )(tok, attn_gain, mlp_gain, lengths, live_mask, w_qkv, keys, values, w_out, w_gate, w_up, w_down)


def per_device(
    tokens,
    attn_gain,
    qkv_weight,
    cache_keys,
    cache_values,
    lengths,
    live_mask,
    out_weight,
    mlp_gain,
    gate_weight,
    up_weight,
    down_weight,
):
    base, extra = layer_rows(
        tokens,
        attn_gain,
        mlp_gain,
        lengths,
        live_mask,
        qkv_weight,
        cache_keys.reshape(cache_keys.shape[0], *cache_keys.shape[2:]),
        cache_values.reshape(cache_values.shape[0], *cache_values.shape[2:]),
        out_weight,
        gate_weight,
        up_weight,
        down_weight,
    )
    return (base.astype(F32) + extra).astype(BF16)


def solution(mesh):
    finer = Mesh(mesh.devices.reshape(4, 4, 4, 2), ("x", "z", "y", "c"))
    return jax.shard_map(
        per_device,
        mesh=finer,
        in_specs=(
            P(None, GX),
            P(GX),
            P(GX, GY),
            P(GX, GY, None, None),
            P(GX, GY, None, None),
            P(),
            P(),
            P(GY, GX),
            P(GX),
            P(GX, GY),
            P(GX, GY),
            P(GY, GX),
        ),
        out_specs=P(GY, GX),
        check_vma=False,
    )
```

time: 373 us -> 123 us (0.33)
  waiting for transfers between devices: 277 us -> 0 us
  Pallas kernels: 0 us -> 121 us
  blocking collectives: 35.4 us -> 0 us
  matrix products: 21.1 us -> 0 us
  other arithmetic: 20.5 us -> 1.55 us
  between operations: 13.4 us -> 0.01 us
  starting transfers between devices: 5.55 us -> 0 us
    reduce_scatter x2 -> x0, waiting for transfers between devices: 161 us -> none  [the longest x1 84.3 us: per_device(): lax.psum_scatter(jnp.concatenate((jnp.dot(mlp_in, gate_weight, preferred_...]
    pallas_call x0 -> x1, Pallas kernels: none -> 121 us  [layer_rows(): pl.pallas_call(layer_kernel, name='layer_rows', out_shape=(jax.ShapeDtype...]
    all_gather x2 -> x0, waiting for transfers between devices: 100 us -> none  [the longest x1 52 us: gathered_total(): parts = lax.all_gather(value, axis)]
    dot_general x8 -> x0, matrix products: 21.1 us -> none  [the longest x1 6.26 us: per_device(): jnp.dot(lax.all_gather(hidden_share, GX, axis=0, tiled=True), down_weight...]
    psum x2 -> x0, blocking collectives: 17.9 us -> none  [over_axes(): return functools.reduce(lax.psum, axes, value)]
    all_to_all x1 -> x0, blocking collectives: 17.5 us -> none  [from_everyone(): lax.all_to_all(jnp.broadcast_to(value[None], (length, *value.shape)), axi...]
    all_to_all x1 -> x0, waiting for transfers between devices: 14.9 us -> none  [sent_and_summed(): lax.all_to_all(cut_along(value, dim, length), axis, 0, 0, tiled=True)]
    concatenate x4 -> x0, other arithmetic: 7.48 us -> none  [the longest x1 5.49 us: per_device(): jnp.concatenate((jnp.dot(mlp_in, gate_weight, preferred_element_type=jnp....]
  transfers between devices with their start and end apart: 5 -> 0, of which waited for: 5 -> 0; matrix products, arithmetic and copies ran while one was open for 0% -> 0% of each run, Pallas kernels for 0% -> 0%
where the time goes in v1:
time: 123 us
  Pallas kernels  121 us (98%)
  other arithmetic  1.55 us (1%)
    pallas_call x1, Pallas kernels, layer_rows(): pl.pallas_call(layer_kernel, name='layer_rows', out_shape=(jax.ShapeDtype...  121 us

profile of v1, /device:TPU:1, one launch (start us, length us, event | category | flops | bytes accessed | tf_op | source)
XLA Modules:
  0.0 122.6 jit_solution(9109684854430809733)
XLA Ops:
  0.0 121.1 %layer_rows.1 = (bf16[64,512]{1,0:T(8,128)(2,1)}, f32[64,512]{1,0:T(8,128)}) custom-call(bf16[512,512]{1,0:T(8,128)(2,1)} %tok.1, bf16[512]{0:T(512)(128)(2,1)} %attn_gain.1, bf16[512]{0:T(512)(128)(2,1)} %mlp_gain.1, s32[512]{0:T(512)} %lengths.1, s32[512]{0:T(512)} %live_mask.1, bf16[512,1280]{1,0:T(8,128)(2,1)} %w_qkv.1, bf16[32,512,128]{2,1,0:T(8,128)(2,1)} %bitcast.2, ...), custom_call_target="tpu_custom_call" | custom-call | tf_op jit(solution)/shard_map/layer_rows/pallas_call | solution.py:775
  121.1 1.6 %add_convert_fusion = bf16[64,512]{1,0:T(8,128)(2,1)} fusion(f32[64,512]{1,0:T(8,128)} %get-tuple-element.8, bf16[64,512]{1,0:T(8,128)(2,1)} %get-tuple-element.7), kind=kLoop, calls=%fused_computation | loop fusion | flops 98304 | bytes 262144 | tf_op jit(solution)/shard_map/convert_element_type | solution.py:852

commit v2 on v1

--- a/solution.py
+++ b/solution.py
@@ -186,7 +186,7 @@
 def run_stages(count, stages):
     def body(t, carry):
         for lag, stage in enumerate(stages):
-            k = t - lag
+            k = t - 2 * lag
 
             @pl.when((k >= 0) & (k < count))
             def _():
@@ -194,7 +194,7 @@
 
         return carry
 
-    lax.fori_loop(0, count + len(stages) - 1, body, 0)
+    lax.fori_loop(0, count + 2 * len(stages) - 2, body, 0)
 
 
 def scatter_stages(rings, part, far1, near1, sum1, far2, near2, ssem, rsem):
@@ -221,11 +221,10 @@
 
     chunks = part.shape[1]
 
-    def start1(k):
+    def start1(h, k):
         def work(direct):
-            for h in range(2):
-                refs = (block1(h, k), far_in1(h, k), near_in1(h, k))
-                scatter_start(rings[h], *refs, ssem.at[k, h, 0], rs(h, k, 0), direct)
+            refs = (block1(h, k), far_in1(h, k), near_in1(h, k))
+            scatter_start(rings[h], *refs, ssem.at[k, h, 0], rs(h, k, 0), direct)
 
         either(k, chunks, STRAIGHT[0], work)
 
@@ -346,17 +345,23 @@
 
 def columns_sum(acc, full, mine, core_in, ring, y_in, ssem, rsem):
     core = lax.axis_index("c")
-    for b in range(16):
-        a, c = divmod(b, 4)
-        both = acc[0, a, c] + acc[1, c, a]
-        full[(b // 2) % 2, b // 4, pl.ds(32 * (b % 2), 32)] = both.astype(BF16)
+
+    def made(c, y):
+        rows = []
+        for i in range(2):
+            z = 2 * c + i
+            rows.append(acc[0, y, z] + acc[1, z, y])
+        return jnp.concatenate(rows, axis=0)
+
     for r in (2, 1, 3, 0):
         place = ring.places[r]
-        send(full.at[1 - core, place], core_in.at[place], ssem.at[0], rsem.at[r], {"c": 1 - core})
+        full[place] = made(1 - core, place).astype(BF16)
+        send(full.at[place], core_in.at[place], ssem.at[0], rsem.at[r], {"c": 1 - core})
     for r in (2, 1, 3, 0):
         place = ring.places[r]
+        both = made(core, place)
         wait_bytes(core_in.at[place], rsem.at[r])
-        both = full[core, place].astype(F32) + core_in[place].astype(F32)
+        both = both + core_in[place].astype(F32)
         if r == 0:
             total = both
         else:
@@ -369,34 +374,44 @@
     return total
 
 
-def gather_plane(rings, buf, ssem, rsem):
-    def block(h, r):
-        return buf.at[h, rings[h].me, rings[1 - h].places[r]]
-
-    def outward(h, r):
+class PlaneGather:
+    def __init__(self, rings, buf, ssem, rsem):
+        self.rings, self.buf, self.ssem, self.rsem = rings, buf, ssem, rsem
+
+    def block(self, h, r, piece):
+        place = self.rings[1 - h].places[r]
+        return self.buf.at[h, self.rings[h].me, place, pl.ds(16 * piece, 16)]
+
+    def outward(self, h, r, piece):
+        ref = self.block(h, r, piece)
         for way in (2, 1, 3):
-            send(block(h, r), block(h, r), ssem.at[h], rsem.at[h, 2 + way], rings[h].devices[way])
-
-    for h in range(2):
-        for way in (2, 1, 3):
-            device = rings[1 - h].devices[way]
-            send(block(h, 0), block(h, 0), ssem.at[h], rsem.at[h, way - 1], device)
-    for h in range(2):
-        outward(h, 0)
-    for way in (1, 3, 2):
+            device = self.rings[h].devices[way]
+            send(ref, ref, self.ssem.at[h, piece], self.rsem.at[h, piece, 2 + way], device)
+
+    def start(self, piece):
         for h in range(2):
-            wait_bytes(block(h, 4 - way), rsem.at[h, way - 1])
-            outward(h, 4 - way)
-
-    def finish(h):
+            ref = self.block(h, 0, piece)
+            for way in (2, 1, 3):
+                device = self.rings[1 - h].devices[way]
+                send(ref, ref, self.ssem.at[h, piece], self.rsem.at[h, piece, way - 1], device)
+        for h in range(2):
+            self.outward(h, 0, piece)
+
+    def relay(self, piece):
         for way in (1, 3, 2):
-            wait_bytes(buf.at[h, rings[h].places[4 - way]], rsem.at[h, 2 + way])
-
-    def drain(h):
-        wait_bytes(buf.at[h, 0, pl.ds(0, 3)], ssem.at[h])
-        wait_bytes(buf.at[h, pl.ds(0, 3)], ssem.at[h])
-
-    return finish, drain
+            for h in range(2):
+                wait_bytes(self.block(h, 4 - way, piece), self.rsem.at[h, piece, way - 1])
+                self.outward(h, 4 - way, piece)
+
+    def finish(self, h, way, piece):
+        place = self.rings[h].places[4 - way]
+        wait_bytes(self.buf.at[h, place, :, pl.ds(16 * piece, 16)], self.rsem.at[h, piece, 2 + way])
+
+    def drain(self):
+        for h in range(2):
+            for piece in range(2):
+                wait_bytes(self.buf.at[h, 0, pl.ds(0, 3), pl.ds(0, 16)], self.ssem.at[h, piece])
+                wait_bytes(self.buf.at[h, pl.ds(0, 3), :, pl.ds(0, 16)], self.ssem.at[h, piece])
 
 
 def rotation(places):
@@ -431,10 +446,14 @@
     v_gate,
     v_up,
     v_down,
-    q_part,
-    q_in1,
-    q_sum1,
-    q_in2,
+    qa_part,
+    qa_in1,
+    qa_sum1,
+    qa_in2,
+    qb_part,
+    qb_in1,
+    qb_sum1,
+    qb_in2,
     sq0,
     sq0_x,
     sq0_mid,
@@ -512,8 +531,7 @@
     def row(ref):
         return ref[...].astype(F32).reshape(1, ref.shape[0])
 
-    def normed(a, wide, gain, squares):
-        squares[a] = row_squares(wide)
+    def normed(a, wide, gain):
         scaled = (wide * gain).astype(BF16).reshape(4, 32, depth)
         lhs[0, a] = scaled
         for b in range(4):
@@ -521,61 +539,71 @@
 
     loads[0].wait()
     for a in range(4):
-        normed(a, v_tok[128 * a : 128 * (a + 1), :].astype(F32), row(attn_gain), sq0)
+        normed(a, v_tok[128 * a : 128 * (a + 1), :].astype(F32), row(attn_gain))
     loads[1].wait()
     for load in loads[2:]:
         load.start()
-    q_width = q_part.shape[4]
-    for h in range(2):
-        columns = slice(h * q_width, (h + 1) * q_width)
-        got = jnp.dot(lhs[h].reshape(512, depth), v_qkv[:, columns], preferred_element_type=F32)
-        q_part[h] = got.astype(BF16).reshape(4, 4, 32, q_width)
     squares0 = Squares(rings, sq0, sq0_x, sq0_mid, sq0_z, sqs0)
     squares = Squares(rings, sq, sq_x, sq_mid, sq_z, sqs)
-    met()
-    for h in range(2):
-        scatter_direct(
-            rings[h],
-            lambda d: q_part.at[h, d],
-            lambda i: q_in1.at[h, i],
-            q_ssem.at[h, 0],
-            q_rsem.at[h, 0],
-        )
+    pieces = (
+        (qa_part, qa_in1, qa_sum1, qa_in2, 0, 3),
+        (qb_part, qb_in1, qb_sum1, qb_in2, 3, 5),
+    )
+    for p, (q_part, q_in1, _, _, begin, end) in enumerate(pieces):
+        width_q = HD * (end - begin)
+        for h in range(2):
+            columns = slice(HD * (5 * h + begin), HD * (5 * h + end))
+            got = jnp.dot(lhs[h].reshape(512, depth), v_qkv[:, columns], preferred_element_type=F32)
+            q_part[h] = got.astype(BF16).reshape(4, 4, 32, width_q)
+            if p == 0 and h == 0:
+                met()
+            scatter_direct(
+                rings[h],
+                lambda d: q_part.at[h, d],
+                lambda i: q_in1.at[h, i],
+                q_ssem.at[p, h, 0],
+                q_rsem.at[p, h, 0],
+            )
+    for a in range(4):
+        sq0[a] = row_squares(v_tok[128 * a : 128 * (a + 1), :].astype(F32))
     squares0.over_x()
     places = as_column(row(lengths), 32, slot0)
     cosine, sine = rotation(places)
-    squares0.over_z()
-    for h in range(2):
-        wait_bytes(q_in1.at[h], q_rsem.at[h, 0])
-        total = q_part[h, rings[h].me].astype(F32)
-        for i in range(3):
-            total = total + q_in1[h, i].astype(F32)
-        q_sum1[h] = total.astype(BF16)
-        scatter_direct(
-            rings[1 - h],
-            lambda d: q_sum1.at[h, d],
-            lambda i: q_in2.at[h, i],
-            q_ssem.at[h, 1],
-            q_rsem.at[h, 1],
-        )
+    fresh[:, 2, :] = jnp.broadcast_to(places, (32, 128))
+    for p, (q_part, q_in1, q_sum1, q_in2, _, _) in enumerate(pieces):
+        for h in range(2):
+            wait_bytes(q_in1.at[h], q_rsem.at[p, h, 0])
+            total = q_part[h, rings[h].me].astype(F32)
+            for i in range(3):
+                total = total + q_in1[h, i].astype(F32)
+            q_sum1[h] = total.astype(BF16)
+            scatter_direct(
+                rings[1 - h],
+                lambda d: q_sum1.at[h, d],
+                lambda i: q_in2.at[h, i],
+                q_ssem.at[p, h, 1],
+                q_rsem.at[p, h, 1],
+            )
+        if p == 0:
+            squares0.over_z()
     scale = squares0.scale()
-    for h in range(2):
-        wait_bytes(q_in2.at[h], q_rsem.at[h, 1])
-        total = q_sum1[h, rings[1 - h].me].astype(F32)
-        for i in range(3):
-            total = total + q_in2[h, i].astype(F32)
-        sums = total * scale
-        for i in range(5):
-            column = sums[:, 128 * i : 128 * (i + 1)]
-            head = 5 * h + i
-            if head < 9:
-                column = column * cosine + pltpu.roll(column, HD // 2, 1) * sine
-            column = column.astype(BF16).astype(F32)
-            if head < 8:
-                query[:, head, :] = column
-            else:
-                fresh[:, head - 8, :] = column
-    fresh[:, 2, :] = jnp.broadcast_to(places, (32, 128))
+    for p, (_, _, q_sum1, q_in2, begin, end) in enumerate(pieces):
+        for h in range(2):
+            wait_bytes(q_in2.at[h], q_rsem.at[p, h, 1])
+            total = q_sum1[h, rings[1 - h].me].astype(F32)
+            for i in range(3):
+                total = total + q_in2[h, i].astype(F32)
+            sums = total * scale
+            for i in range(end - begin):
+                column = sums[:, 128 * i : 128 * (i + 1)]
+                head = 5 * h + begin + i
+                if head < 9:
+                    column = column * cosine + pltpu.roll(column, HD // 2, 1) * sine
+                column = column.astype(BF16).astype(F32)
+                if head < 8:
+                    query[:, head, :] = column
+                else:
+                    fresh[:, head - 8, :] = column
 
     loads[2].wait()
     loads[3].wait()
@@ -623,19 +651,24 @@
         attended[pl.ds(first, 8)] = (blend / totals).reshape(8, 8, HD)
         return carry
 
-    lax.fori_loop(0, 4, slots, 0)
-    for head in range(8):
-        h, i = divmod(head, 4)
-        abuf[h, rings[h].me, rings[1 - h].me, :, 128 * i : 128 * (i + 1)] = attended[
-            :, head, :
-        ].astype(BF16)
-
-    a_finish, a_drain = gather_plane(rings, abuf, a_ssem, a_rsem)
+    gather = PlaneGather(rings, abuf, a_ssem, a_rsem)
+    for piece in range(2):
+        lax.fori_loop(2 * piece, 2 * piece + 2, slots, 0)
+        rows = pl.ds(16 * piece, 16)
+        for head in range(8):
+            h, i = divmod(head, 4)
+            abuf[h, rings[h].me, rings[1 - h].me, rows, 128 * i : 128 * (i + 1)] = attended[
+                rows, head, :
+            ].astype(BF16)
+        gather.start(piece)
+    for piece in range(2):
+        gather.relay(piece)
+    half = abuf.shape[4]
+    loads[4].wait()
     for h in range(2):
-        a_finish(h)
-        if h == 0:
-            loads[4].wait()
-        half = abuf.shape[4]
+        for piece in range(2):
+            for way in (1, 3, 2):
+                gather.finish(h, way, piece)
         block = abuf[h].reshape(512, half)
         got = jnp.dot(block, v_out[h * half : (h + 1) * half, :], preferred_element_type=F32)
         acc[h] = got.reshape(4, 4, 32, acc.shape[4])
@@ -646,21 +679,25 @@
     def r_whole(d):
         return resid.at[d, core]
 
-    def to_core(d):
-        send(r_whole(d), r_whole(d), r_ssem.at[1], r_rsem.at[3], {"c": 1 - core})
+    def to_core(r):
+        ref = r_whole(yring.places[r])
+        send(ref, ref, r_ssem.at[1], r_rsem.at[3 + r], {"c": 1 - core})
+
+    def take(r):
+        place = yring.places[r]
+        wait_bytes(resid.at[place, 1 - core], r_rsem.at[3 + r])
+        normed(place, resid[place].astype(F32).reshape(128, depth), row(mlp_gain))
 
     resid[yring.me, core] = kept
     gather_direct(yring, r_whole, r_ssem.at[0], lambda i: r_rsem.at[i])
-    to_core(yring.me)
+    to_core(0)
+    acc[...] = jnp.zeros_like(acc)
+    take(0)
     for r in (1, 3, 2):
         wait_bytes(r_whole(yring.places[4 - r]), r_rsem.at[r - 1])
-        to_core(yring.places[4 - r])
-    wait_bytes(resid.at[:, 1 - core], r_rsem.at[3])
-
-    for a in range(4):
-        normed(a, resid[a].astype(F32).reshape(128, depth), row(mlp_gain), sq)
-    squares.over_x()
-    acc[...] = jnp.zeros_like(acc)
+        to_core(4 - r)
+    for r in (1, 3, 2):
+        take(4 - r)
     for load in loads[5:]:
         load.wait()
 
@@ -683,7 +720,13 @@
                 part[h, k, :, :, :, i * cut : (i + 1) * cut] = got.astype(BF16).reshape(
                     4, 4, 32, cut
                 )
-        s_start1(k)
+            s_start1(h, k)
+
+        @pl.when(k == 0)
+        def _():
+            for a in range(4):
+                sq[a] = row_squares(resid[a].astype(F32).reshape(128, depth))
+            squares.over_x()
 
     def hidden(k):
         @pl.when(k == 0)
@@ -733,10 +776,11 @@
 
     squares0.drain()
     squares.drain()
-    for h in range(2):
-        a_drain(h)
-        wait_bytes(q_in1.at[h], q_ssem.at[h, 0])
-        wait_bytes(q_in2.at[h], q_ssem.at[h, 1])
+    gather.drain()
+    for p, (_, q_in1, _, q_in2, _, _) in enumerate(pieces):
+        for h in range(2):
+            wait_bytes(q_in1.at[h], q_ssem.at[p, h, 0])
+            wait_bytes(q_in2.at[h], q_ssem.at[p, h, 1])
     wait_bytes(resid.at[pl.ds(0, 3), 0], r_ssem.at[0])
     wait_bytes(resid.at[:, 0], r_ssem.at[1])
 
@@ -750,13 +794,21 @@
     lax.fori_loop(0, chunks, drain, 0)
 
 
+def q_scratch(width):
+    return [
+        pltpu.VMEM((2, 4, 4, 32, width), BF16),
+        pltpu.VMEM((2, 3, 4, 32, width), BF16),
+        pltpu.VMEM((2, 4, 32, width), BF16),
+        pltpu.VMEM((2, 3, 32, width), BF16),
+    ]
+
+
 def layer_rows(tok, attn_gain, mlp_gain, lengths, live_mask, w_qkv, keys, values, w_out, w_gate, w_up, w_down):
     depth = w_gate.shape[0]
     cut = w_gate.shape[1] // (2 * MLP_CHUNKS)
     half = w_out.shape[0] // 2
     across = w_out.shape[1]
     slots = keys.shape[0]
-    q_width = w_qkv.shape[1] // 2
     vmem = pl.BlockSpec(memory_space=pltpu.VMEM)
     hbm = pl.BlockSpec(memory_space=pl.ANY)
     held = (tok, w_qkv, keys, values, w_out, w_gate, w_up, w_down)
@@ -767,7 +819,7 @@
         pltpu.VMEM((3, 8, 128), F32),
     ]
     sums = [
-        pltpu.VMEM((2, 4, 64, across), BF16),
+        pltpu.VMEM((4, 64, across), BF16),
         pltpu.VMEM((4, 64, across), BF16),
         pltpu.VMEM((4, 64, across), BF16),
         pltpu.VMEM((3, 64, across), BF16),
@@ -783,10 +835,8 @@
         out_specs=(vmem, vmem),
         scratch_shapes=[
             *[pltpu.VMEM(a.shape, BF16) for a in held],
-            pltpu.VMEM((2, 4, 4, 32, q_width), BF16),
-            pltpu.VMEM((2, 3, 4, 32, q_width), BF16),
-            pltpu.VMEM((2, 4, 32, q_width), BF16),
-            pltpu.VMEM((2, 3, 32, q_width), BF16),
+            *q_scratch(3 * HD),
+            *q_scratch(2 * HD),
             *squares,
             pltpu.VMEM((slots, 8, HD), F32),
             pltpu.VMEM((slots, 8, HD), F32),
@@ -802,15 +852,15 @@
             *squares,
             pltpu.VMEM((32, 128), F32),
             pltpu.SemaphoreType.DMA((8,)),
+            pltpu.SemaphoreType.DMA((2, 2, 2)),
+            pltpu.SemaphoreType.DMA((2, 2, 2)),
+            pltpu.SemaphoreType.DMA((4,)),
             pltpu.SemaphoreType.DMA((2, 2)),
-            pltpu.SemaphoreType.DMA((2, 2)),
-            pltpu.SemaphoreType.DMA((4,)),
-            pltpu.SemaphoreType.DMA((2,)),
-            pltpu.SemaphoreType.DMA((2, 6)),
+            pltpu.SemaphoreType.DMA((2, 2, 6)),
             pltpu.SemaphoreType.DMA((2, 2)),
             pltpu.SemaphoreType.DMA((2, 5)),
             pltpu.SemaphoreType.DMA((2,)),
-            pltpu.SemaphoreType.DMA((4,)),
+            pltpu.SemaphoreType.DMA((7,)),
             pltpu.SemaphoreType.DMA((4,)),
             pltpu.SemaphoreType.DMA((MLP_CHUNKS, 2, 4)),
             pltpu.SemaphoreType.DMA((MLP_CHUNKS, 2, 16)),

time: 123 us -> 120 us (0.976)
  Pallas kernels: 121 us -> 119 us
    pallas_call x1, Pallas kernels: 121 us -> 119 us  [layer_rows(): pl.pallas_call(layer_kernel, name='layer_rows', out_shape=(jax.ShapeDtype...]
where the time goes in v2:
time: 120 us
  Pallas kernels  119 us (99%)
  other arithmetic  1.55 us (1%)
    pallas_call x1, Pallas kernels, layer_rows(): pl.pallas_call(layer_kernel, name='layer_rows', out_shape=(jax.ShapeDtype...  119 us

profile of v2, /device:TPU:1, one launch (start us, length us, event | category | flops | bytes accessed | tf_op | source)
XLA Modules:
  0.0 120.2 jit_solution(12338351131889956159)
XLA Ops:
  0.0 118.6 %layer_rows.1 = (bf16[64,512]{1,0:T(8,128)(2,1)}, f32[64,512]{1,0:T(8,128)}) custom-call(bf16[512,512]{1,0:T(8,128)(2,1)} %tok.1, bf16[512]{0:T(512)(128)(2,1)} %attn_gain.1, bf16[512]{0:T(512)(128)(2,1)} %mlp_gain.1, s32[512]{0:T(512)} %lengths.1, s32[512]{0:T(512)} %live_mask.1, bf16[512,1280]{1,0:T(8,128)(2,1)} %w_qkv.1, bf16[32,512,128]{2,1,0:T(8,128)(2,1)} %bitcast.2, ...), custom_call_target="tpu_custom_call" | custom-call | tf_op jit(solution)/shard_map/layer_rows/pallas_call | solution.py:827
  118.6 1.6 %add_convert_fusion = bf16[64,512]{1,0:T(8,128)(2,1)} fusion(f32[64,512]{1,0:T(8,128)} %get-tuple-element.8, bf16[64,512]{1,0:T(8,128)(2,1)} %get-tuple-element.7), kind=kLoop, calls=%fused_computation | loop fusion | flops 98304 | bytes 262144 | tf_op jit(solution)/shard_map/convert_element_type | solution.py:902

commit v3 on v2

--- a/solution.py
+++ b/solution.py
@@ -343,7 +343,7 @@
     return start1, forward1, start2, forward2, finish2, drain
 
 
-def columns_sum(acc, full, mine, core_in, ring, y_in, ssem, rsem):
+def columns_sum(acc, full, mine, core_in, ring, y_in, ssem, rsem, meanwhile=None):
     core = lax.axis_index("c")
 
     def made(c, y):
@@ -367,6 +367,8 @@
         else:
             mine[place] = both.astype(BF16)
             send(mine.at[place], y_in.at[r - 1], ssem.at[1], rsem.at[4], ring.devices[r])
+    if meanwhile is not None:
+        meanwhile()
     wait_bytes(y_in, rsem.at[4])
     total = total + jnp.sum(y_in[...].astype(F32), axis=0)
     wait_bytes(core_in, ssem.at[0])
@@ -425,10 +427,10 @@
 
 def layer_kernel(
     tok,
-    attn_gain,
-    mlp_gain,
-    lengths,
-    live_mask,
+    h_attn_gain,
+    h_mlp_gain,
+    h_lengths,
+    h_live_mask,
     w_qkv,
     keys,
     values,
@@ -438,6 +440,10 @@
     w_down,
     base,
     extra,
+    attn_gain,
+    mlp_gain,
+    lengths,
+    live_mask,
     v_tok,
     v_qkv,
     v_keys,
@@ -522,7 +528,20 @@
             )
         )
     ]
+    small = [
+        pltpu.make_async_copy(src, dst, wsem.at[8 + i])
+        for i, (src, dst) in enumerate(
+            (
+                (h_attn_gain, attn_gain),
+                (h_mlp_gain, mlp_gain),
+                (h_lengths, lengths),
+                (h_live_mask, live_mask),
+            )
+        )
+    ]
     loads[0].start()
+    for load in small:
+        load.start()
     loads[1].start()
     met = greet(
         [*rings[0].devices[1:], *rings[1].devices[1:], *yring.devices[1:], {"c": 1 - core}]
@@ -537,6 +556,8 @@
         for b in range(4):
             lhs[1, b, a] = scaled[b]
 
+    for load in small:
+        load.wait()
     loads[0].wait()
     for a in range(4):
         normed(a, v_tok[128 * a : 128 * (a + 1), :].astype(F32), row(attn_gain))
@@ -722,7 +743,7 @@
                 )
             s_start1(h, k)
 
-        @pl.when(k == 0)
+        @pl.when(k == 1)
         def _():
             for a in range(4):
                 sq[a] = row_squares(resid[a].astype(F32).reshape(128, depth))
@@ -759,7 +780,7 @@
             acc[h] += got.reshape(4, 4, 32, acc.shape[4])
 
     def forward1(k):
-        @pl.when(k == 0)
+        @pl.when(k == 1)
         def _():
             squares.over_z()
 
@@ -770,28 +791,30 @@
         (compute, forward1, s_start2, s_forward2, hidden, g_forward1, g_start2, g_forward2, down),
     )
 
-    total = columns_sum(acc, full2, mine2, core_in2, yring, y_in2, y_ssem.at[1], y_rsem.at[1])
+    def settle():
+        squares0.drain()
+        squares.drain()
+        gather.drain()
+        for p, (_, q_in1, _, q_in2, _, _) in enumerate(pieces):
+            for h in range(2):
+                wait_bytes(q_in1.at[h], q_ssem.at[p, h, 0])
+                wait_bytes(q_in2.at[h], q_ssem.at[p, h, 1])
+        wait_bytes(resid.at[pl.ds(0, 3), 0], r_ssem.at[0])
+        wait_bytes(resid.at[:, 0], r_ssem.at[1])
+
+        def drain(k, carry):
+            for h in range(2):
+                wait_bytes(part.at[h, k, pl.ds(0, 3)], m_ssem.at[k, h, 0])
+                wait_bytes(sum1.at[h, k, pl.ds(0, 3)], m_ssem.at[k, h, 1])
+                g_drain(h, k)
+            return carry
+
+        lax.fori_loop(0, chunks, drain, 0)
+
+    sems = (y_ssem.at[1], y_rsem.at[1])
+    total = columns_sum(acc, full2, mine2, core_in2, yring, y_in2, *sems, settle)
     base[...] = kept
     extra[...] = live * total
-
-    squares0.drain()
-    squares.drain()
-    gather.drain()
-    for p, (_, q_in1, _, q_in2, _, _) in enumerate(pieces):
-        for h in range(2):
-            wait_bytes(q_in1.at[h], q_ssem.at[p, h, 0])
-            wait_bytes(q_in2.at[h], q_ssem.at[p, h, 1])
-    wait_bytes(resid.at[pl.ds(0, 3), 0], r_ssem.at[0])
-    wait_bytes(resid.at[:, 0], r_ssem.at[1])
-
-    def drain(k, carry):
-        for h in range(2):
-            wait_bytes(part.at[h, k, pl.ds(0, 3)], m_ssem.at[k, h, 0])
-            wait_bytes(sum1.at[h, k, pl.ds(0, 3)], m_ssem.at[k, h, 1])
-            g_drain(h, k)
-        return carry
-
-    lax.fori_loop(0, chunks, drain, 0)
 
 
 def q_scratch(width):
@@ -831,9 +854,10 @@
             jax.ShapeDtypeStruct((64, across), BF16),
             jax.ShapeDtypeStruct((64, across), F32),
         ),
-        in_specs=[hbm] + [vmem] * 4 + [hbm] * 7,
+        in_specs=[hbm] * 12,
         out_specs=(vmem, vmem),
         scratch_shapes=[
+            *[pltpu.VMEM(a.shape, a.dtype) for a in (attn_gain, mlp_gain, lengths, live_mask)],
             *[pltpu.VMEM(a.shape, BF16) for a in held],
             *q_scratch(3 * HD),
             *q_scratch(2 * HD),
@@ -851,7 +875,7 @@
             pltpu.VMEM((2, MLP_CHUNKS, 4, 4, 32, cut), BF16),
             *squares,
             pltpu.VMEM((32, 128), F32),
-            pltpu.SemaphoreType.DMA((8,)),
+            pltpu.SemaphoreType.DMA((12,)),
             pltpu.SemaphoreType.DMA((2, 2, 2)),
             pltpu.SemaphoreType.DMA((2, 2, 2)),
             pltpu.SemaphoreType.DMA((4,)),

time: 120 us -> 120 us (level)
  no operation moved by 1% of the time
where the time goes in v3:
time: 120 us; the launch traced here: 119 us
  Pallas kernels  118 us (98%)
  other arithmetic  1.55 us (1%)
    pallas_call x1, Pallas kernels, layer_rows(): pl.pallas_call(layer_kernel, name='layer_rows', out_shape=(jax.ShapeDtype...  118 us

profile of v3, /device:TPU:1, one launch (start us, length us, event | category | flops | bytes accessed | tf_op | source)
XLA Modules:
  0.0 119.4 jit_solution(10790038847203501899)
XLA Ops:
  0.0 117.8 %layer_rows.1 = (bf16[64,512]{1,0:T(8,128)(2,1)}, f32[64,512]{1,0:T(8,128)}) custom-call(bf16[512,512]{1,0:T(8,128)(2,1)} %tok.1, bf16[512]{0:T(512)(128)(2,1)} %h_attn_gain.1, bf16[512]{0:T(512)(128)(2,1)} %h_mlp_gain.1, s32[512]{0:T(512)} %h_lengths.1, s32[512]{0:T(512)} %h_live_mask.1, bf16[512,1280]{1,0:T(8,128)(2,1)} %w_qkv.1, ...), custom_call_target="tpu_custom_call" | custom-call | tf_op jit(solution)/shard_map/layer_rows/pallas_call | solution.py:850
  117.8 1.6 %add_convert_fusion = bf16[64,512]{1,0:T(8,128)(2,1)} fusion(f32[64,512]{1,0:T(8,128)} %get-tuple-element.8, bf16[64,512]{1,0:T(8,128)(2,1)} %get-tuple-element.7), kind=kLoop, calls=%fused_computation | loop fusion | flops 98304 | bytes 262144 | tf_op jit(solution)/shard_map/convert_element_type | solution.py:926
